TPU v7x, 32 devices: a whole 2x2x4 slice. The times are simulated.
32 devices in a mesh: owner: 4 (over y, core), rows: 8 (over z, x).
Axes of the slice: x: 2, y: 2, z: 4, core: 2. Of those that a mesh axis runs over, the one named last changes fastest.
Arguments:
- train_gate: float32 [128, 2048, 768], P('owner', 'rows'), may hold values from -0.125 to 0.125
- train_up: float32 [128, 2048, 768], P('owner', 'rows'), may hold values from -0.125 to 0.125
- router_weight: float32 [2048, 128], P('rows', 'owner'), may hold values from -0.125 to 0.125
- router_gain: float32 [2048], P('rows'), may hold values from 0.25 to 1.75
Outputs:
- ready_gate: bfloat16 [128, 768, 2048], P(('owner', 'rows'))
- ready_up: bfloat16 [128, 768, 2048], P(('owner', 'rows'))
- serve_router: bfloat16 [2048, 128], replicated
All inputs are finite; a program needn't handle non-finite values.
Results may differ from a plain program's by a relative error of at most 0.001.
Values may be sent and summed in bfloat16 or wider, within the bound.
A program may use at most 192 MiB of HBM per device.

v0:
```python
import jax
import jax.numpy as jnp
from jax import lax
from jax.sharding import PartitionSpec as P


def on_device(train_gate, train_up, router_weight, router_gain):
    narrow_gate, narrow_up = (train_gate.astype(jnp.bfloat16), train_up.astype(jnp.bfloat16))
    ready_gate, ready_up = (
        lax.all_to_all(narrow_gate, "rows", split_axis=0, concat_axis=1, tiled=True),
        lax.all_to_all(narrow_up, "rows", split_axis=0, concat_axis=1, tiled=True),
    )
    ready_gate = jnp.transpose(ready_gate, (0, 2, 1))
    ready_up = jnp.transpose(ready_up, (0, 2, 1))
    part_router = (router_weight * router_gain[:, None]).astype(jnp.bfloat16)
    row_router = lax.all_gather(part_router, "rows", axis=0, tiled=True)
    serve_router = lax.all_gather(row_router, "owner", axis=1, tiled=True)
    return (ready_gate, ready_up, serve_router)


def solution(mesh):
    placed = (P("owner", "rows", None), P("owner", "rows", None), P("rows", "owner"), P("rows"))
    return jax.shard_map(
        on_device,
        mesh=mesh,
        in_specs=placed,
        out_specs=(P(("owner", "rows"), None, None), P(("owner", "rows"), None, None), P()),
        check_vma=False,
    )
```

profile of v0, /device:TPU:0, one launch (start us, length us, event | category | flops | bytes accessed | tf_op | source)
XLA Modules:
  0.0 672.7 jit_solution(13268045616997217038)
XLA Ops:
  0.6 13.2 %convert_element_type.9 = bf16[32,256,768]{2,1,0:T(8,128)(2,1)} convert(f32[32,256,768]{2,1,0:T(8,128)} %param.4) | non-fusion elementwise | flops 6291456 | bytes 37748736 | tf_op jit(solution)/shard_map/convert_element_type | solution.py:8
  13.8 7.3 %all-to-all-start = ((bf16[32,256,768]{2,1,0:T(8,128)(2,1)}), bf16[32,256,768]{2,1,0:T(8,128)(2,1)}, u32[]{:S(2)}, u32[]{:S(2)}) async-start(bf16[32,256,768]{2,1,0:T(8,128)(2,1)} %convert_element_type.9), calls=%async_computation | async-start | bytes 25165824 | tf_op jit(solution)/shard_map/all_to_all | solution.py:10
  21.1 13.4 %convert_element_type.10 = bf16[32,256,768]{2,1,0:T(8,128)(2,1)} convert(f32[32,256,768]{2,1,0:T(8,128)} %param.5) | non-fusion elementwise | flops 6291456 | bytes 37748736 | tf_op jit(solution)/shard_map/convert_element_type | solution.py:8
  34.5 0.0 copy-start
  34.5 0.0 copy-start.1
  34.5 259.7 %all-to-all-done = bf16[32,256,768]{2,1,0:T(8,128)(2,1)} async-done(((bf16[32,256,768]{2,1,0:T(8,128)(2,1)}), bf16[32,256,768]{2,1,0:T(8,128)(2,1)}, u32[]{:S(2)}, u32[]{:S(2)}) %all-to-all-start) | async-done | bytes 12582944 | tf_op jit(solution)/shard_map/all_to_all | solution.py:10
  294.2 5.3 all-to-all-start.1
  299.5 0.0 copy-done
  299.5 0.0 copy-done.1
  299.5 292.2 %all_gather.6 = bf16[2048,32]{0,1:T(8,128)(2,1)S(1)} all-gather(bf16[256,32]{0,1:T(8,128)(2,1)S(1)} %multiply_convert_fusion), channel_id=1, replica_groups=mesh['owner'=4,'rows'=8] {'rows'}, dimensions={0}, use_global_device_ids=true | all-gather | bytes 147456 | tf_op jit(solution)/shard_map/all_gather | solution.py:16
  591.8 7.2 %all_gather.7 = bf16[2048,128]{0,1:T(8,128)(2,1)S(1)} all-gather(bf16[2048,32]{0,1:T(8,128)(2,1)S(1)} %all_gather.6), channel_id=1, replica_groups=mesh['owner'=4,'rows'=8] {'owner'}, dimensions={1}, use_global_device_ids=true | all-gather | bytes 655360 | tf_op jit(solution)/shard_map/all_gather | solution.py:17
  598.9 1.0 copy.12
  599.9 16.9 %copy.10 = bf16[8,4,256,768]{2,0,3,1:T(8,128)(2,1)} copy(bf16[8,4,256,768]{3,2,1,0:T(8,128)(2,1)} %bitcast) | data formatting | bytes 25165824 | tf_op jit(solution)/shard_map/all_to_all | solution.py:10
  616.8 19.5 %all_to_all.29 = bf16[4,2048,768]{1,2,0:T(8,128)(2,1)} reshape(bf16[4,8,256,768]{2,1,3,0:T(8,128)(2,1)} %bitcast.14) | data formatting | bytes 25165824 | tf_op jit(solution)/shard_map/all_to_all | solution.py:10
  636.3 0.0 all-to-all-done.1
  636.3 16.9 %copy.11 = bf16[8,4,256,768]{2,0,3,1:T(8,128)(2,1)} copy(bf16[8,4,256,768]{3,2,1,0:T(8,128)(2,1)} %bitcast.3) | data formatting | bytes 25165824 | tf_op jit(solution)/shard_map/all_to_all | solution.py:11
  653.2 19.5 %all_to_all.33 = bf16[4,2048,768]{1,2,0:T(8,128)(2,1)} reshape(bf16[4,8,256,768]{2,1,3,0:T(8,128)(2,1)} %bitcast.15) | data formatting | bytes 25165824 | tf_op jit(solution)/shard_map/all_to_all | solution.py:11
  (1 shorter events, 0.0 us)
Async XLA Ops:
  13.8 280.3 %all-to-all-start = ((bf16[32,256,768]{2,1,0:T(8,128)(2,1)}), bf16[32,256,768]{2,1,0:T(8,128)(2,1)}, u32[]{:S(2)}, u32[]{:S(2)}) async-start(bf16[32,256,768]{2,1,0:T(8,128)(2,1)} %convert_element_type.9), calls=%async_computation | async-start | bytes 25165824 | tf_op jit(solution)/shard_map/all_to_all | solution.py:10
  34.5 265.0 %copy-start = (f32[256,32]{0,1:T(8,128)S(1)}, f32[256,32]{0,1:T(8,128)}, u32[]{:S(2)}) copy-start(f32[256,32]{0,1:T(8,128)} %param.6) | copy-start | bytes 98308
  34.5 265.0 %copy-start.1 = (f32[256]{0:T(256)S(1)}, f32[256]{0:T(256)}, u32[]{:S(2)}) copy-start(f32[256]{0:T(256)} %param.7) | copy-start | bytes 3076
  294.2 342.1 %all-to-all-start.1 = ((bf16[32,256,768]{2,1,0:T(8,128)(2,1)}), bf16[32,256,768]{2,1,0:T(8,128)(2,1)}, u32[]{:S(2)}, u32[]{:S(2)}) async-start(bf16[32,256,768]{2,1,0:T(8,128)(2,1)} %convert_element_type.10), calls=%async_computation.1 | async-start | bytes 25165824 | tf_op jit(solution)/shard_map/all_to_all | solution.py:11
where the time goes:
time: 675 us; the launch traced here: 673 us
  blocking collectives  299 us (44%)
  waiting for transfers between devices  260 us (39%)
  local copies, waits for them, and re-layouts  73.7 us (11%)
  other arithmetic  26.6 us (4%)
  starting transfers between devices  12.6 us (2%)
    all_gather x1, blocking collectives, on_device(): row_router = lax.all_gather(part_router, 'rows', axis=0, tiled=True)  292 us
    all_to_all x1, waiting for transfers between devices, on_device(): lax.all_to_all(narrow_gate, 'rows', split_axis=0, concat_axis=1, tiled=True)  260 us
    all_to_all x2, local copies, waits for them, and re-layouts, on_device(): lax.all_to_all(narrow_up, 'rows', split_axis=0, concat_axis=1, tiled=True)  36.4 us
    all_to_all x2, local copies, waits for them, and re-layouts, on_device(): lax.all_to_all(narrow_gate, 'rows', split_axis=0, concat_axis=1, tiled=True)  36.3 us
  transfers between devices with their start and end apart: 2, of which 1 were waited for; matrix products, arithmetic and copies ran while one was open for 5% of the time, Pallas kernels for 0%

commit v1 on v0

--- a/solution.py
+++ b/solution.py
@@ -4,10 +4,41 @@
 from jax.sharding import PartitionSpec as P
 
 
+def _run_pairs_all(xx, axis_k, mine):
+    field_out = xx.shape
+    current_arr = xx.reshape(
+        *field_out[:axis_k], mine, field_out[axis_k] // mine, *field_out[axis_k + 1 :]
+    )
+    return jnp.moveaxis(current_arr, axis_k, 0)
+
+
+def pass_stocks_now(u, dim_i):
+    seen_now = list(u.shape[1:])
+    seen_now[dim_i] *= u.shape[0]
+    return jnp.moveaxis(u, 0, dim_i).reshape(seen_now)
+
+
 def on_device(train_gate, train_up, router_weight, router_gain):
     narrow_gate, narrow_up = (train_gate.astype(jnp.bfloat16), train_up.astype(jnp.bfloat16))
+
+    def _plan_tokens(own_rows, along_axis, piece_in, payload):
+        n_now = jax.lax.axis_size(along_axis)
+        tall = jax.lax.axis_index(along_axis)
+        view_out, h_now = (n_now, tall)
+        out_arr = _run_pairs_all(piece_in, own_rows, view_out)
+        in_order = [out_arr[h_now]]
+        for i in range(1, view_out):
+            lower = out_arr[(h_now + i) % view_out]
+            item_now = jax.lax.ppermute(
+                lower, along_axis, [(idx, (idx + i) % view_out) for idx in range(view_out)]
+            )
+            in_order.append(item_now)
+        moved = jnp.stack(in_order)
+        out_arr = moved[(h_now - jnp.arange(view_out)) % view_out]
+        return pass_stocks_now(out_arr, payload)
+
     ready_gate, ready_up = (
-        lax.all_to_all(narrow_gate, "rows", split_axis=0, concat_axis=1, tiled=True),
+        _plan_tokens(0, "rows", narrow_gate, 1),
         lax.all_to_all(narrow_up, "rows", split_axis=0, concat_axis=1, tiled=True),
     )
     ready_gate = jnp.transpose(ready_gate, (0, 2, 1))

time: 675 us -> 705 us (1.044)
  waiting for transfers between devices: 260 us -> 52.7 us
  blocking collectives: 299 us -> 505 us
  local copies, waits for them, and re-layouts: 73.7 us -> 101 us
    all_to_all x1 -> x0, waiting for transfers between devices: 260 us -> none  [on_device(): lax.all_to_all(narrow_gate, 'rows', split_axis=0, concat_axis=1, tiled=True)]
    all_gather x1, blocking collectives: 292 us -> 497 us  [on_device(): row_router = lax.all_gather(part_router, 'rows', axis=0, tiled=True)]
    ppermute x0 -> x7, waiting for transfers between devices: none -> 52.7 us  [_plan_tokens(): jax.lax.ppermute(lower, along_axis, [(idx, (idx + i) % view_out) for idx...]
    all_to_all x2 -> x0, local copies, waits for them, and re-layouts: 36.3 us -> none  [on_device(): lax.all_to_all(narrow_gate, 'rows', split_axis=0, concat_axis=1, tiled=True)]
    unnamed x5 -> x12, local copies, waits for them, and re-layouts: 1.01 us -> 32.1 us
    gather x0 -> x1, local copies, waits for them, and re-layouts: none -> 11.2 us  [_plan_tokens(): out_arr = moved[(h_now - jnp.arange(view_out)) % view_out]]
    transpose x0 -> x1, local copies, waits for them, and re-layouts: none -> 10.8 us  [pass_stocks_now(): return jnp.moveaxis(u, 0, dim_i).reshape(seen_now)]
    ppermute x0 -> x7, starting transfers between devices: none -> 10.3 us  [_plan_tokens(): jax.lax.ppermute(lower, along_axis, [(idx, (idx + i) % view_out) for idx...]
  transfers between devices with their start and end apart: 2 -> 8, of which waited for: 1 -> 2; matrix products, arithmetic and copies ran while one was open for 5% -> 11% of each run, Pallas kernels for 0% -> 0%
where the time goes in v1:
time: 705 us; the launch traced here: 703 us
  blocking collectives  505 us (72%)
  local copies, waits for them, and re-layouts  101 us (14%)
  waiting for transfers between devices  52.7 us (7%)
  other arithmetic  26.5 us (4%)
  starting transfers between devices  17.6 us (2%)
    all_gather x1, blocking collectives, on_device(): row_router = lax.all_gather(part_router, 'rows', axis=0, tiled=True)  497 us
    ppermute x7, waiting for transfers between devices, _plan_tokens(): jax.lax.ppermute(lower, along_axis, [(idx, (idx + i) % view_out) for idx...  52.7 us
    all_to_all x2, local copies, waits for them, and re-layouts, on_device(): lax.all_to_all(narrow_up, 'rows', split_axis=0, concat_axis=1, tiled=True)  36.4 us
    unnamed x12, local copies, waits for them, and re-layouts  32.1 us
  transfers between devices with their start and end apart: 8, of which 2 were waited for; matrix products, arithmetic and copies ran while one was open for 11% of the time, Pallas kernels for 0%

profile of v1, /device:TPU:0, one launch (start us, length us, event | category | flops | bytes accessed | tf_op | source)
XLA Modules:
  0.0 702.9 jit_solution(16116264633652682472)
XLA Ops:
  0.6 13.3 %convert_element_type.10 = bf16[32,256,768]{2,1,0:T(8,128)(2,1)} convert(f32[32,256,768]{2,1,0:T(8,128)} %param.5) | non-fusion elementwise | flops 6291456 | bytes 37748736 | tf_op jit(solution)/shard_map/convert_element_type | solution.py:22
  14.0 7.3 %all-to-all-start = ((bf16[32,256,768]{2,1,0:T(8,128)(2,1)}), bf16[32,256,768]{2,1,0:T(8,128)(2,1)}, u32[]{:S(2)}, u32[]{:S(2)}) async-start(bf16[32,256,768]{2,1,0:T(8,128)(2,1)} %convert_element_type.10), calls=%async_computation | async-start | bytes 25165824 | tf_op jit(solution)/shard_map/all_to_all | solution.py:42
  21.2 13.2 %convert_element_type.9 = bf16[32,256,768]{2,1,0:T(8,128)(2,1)} convert(f32[32,256,768]{2,1,0:T(8,128)} %param.4) | non-fusion elementwise | flops 6291456 | bytes 37748736 | tf_op jit(solution)/shard_map/convert_element_type | solution.py:22
  34.4 9.1 %dynamic-slice_bitcast_fusion = (bf16[4,256,768]{2,1,0:T(8,128)(2,1)}, bf16[4,256,768]{2,1,0:T(8,128)(2,1)}, bf16[4,256,768]{2,1,0:T(8,128)(2,1)}, bf16[4,256,76...) fusion(bf16[8,4,256,768]{3,2,1,0:T(8,128)(2,1)} %bitcast.45, ...), kind=kLoop, calls=%fused_computation.8 | loop fusion | bytes 25165856 | tf_op jit(solution)/shard_map/squeeze | solution.py:31
  43.5 2.1 collective-permute-start
  45.6 1.5 collective-permute-start.1
  47.0 2.4 collective-permute-start.2
  49.4 1.5 collective-permute-start.3
  50.9 2.4 collective-permute-start.4
  53.3 497.4 %all_gather.6 = bf16[2048,32]{0,1:T(8,128)(2,1)S(1)} all-gather(bf16[256,32]{0,1:T(8,128)(2,1)S(1)} %multiply_convert_fusion), channel_id=1, replica_groups=mesh['owner'=4,'rows'=8] {'rows'}, dimensions={0}, use_global_device_ids=true | all-gather | bytes 147456 | tf_op jit(solution)/shard_map/all_gather | solution.py:47
  550.7 7.2 %all_gather.7 = bf16[2048,128]{0,1:T(8,128)(2,1)S(1)} all-gather(bf16[2048,32]{0,1:T(8,128)(2,1)S(1)} %all_gather.6), channel_id=1, replica_groups=mesh['owner'=4,'rows'=8] {'owner'}, dimensions={1}, use_global_device_ids=true | all-gather | bytes 655360 | tf_op jit(solution)/shard_map/all_gather | solution.py:48
  557.9 0.0 collective-permute-done
  557.9 0.6 collective-permute-start.5
  558.5 1.0 copy.18
  559.5 0.0 collective-permute-done.1
  559.5 0.0 collective-permute-start.6
  559.5 2.7 bitcast_dynamic-update-slice_fusion.6
  562.1 2.7 bitcast_dynamic-update-slice_fusion.5
  564.8 0.0 collective-permute-done.2
  564.8 2.7 bitcast_dynamic-update-slice_fusion.4
  567.4 0.0 collective-permute-done.3
  567.4 2.7 bitcast_dynamic-update-slice_fusion.3
  570.1 1.2 bitcast_dynamic-update-slice_fusion.2
  571.3 24.1 %collective-permute-done.5 = bf16[4,256,768]{2,1,0:T(8,128)(2,1)} collective-permute-done((bf16[4,256,768]{2,1,0:T(8,128)(2,1)}, bf16[4,256,768]{2,1,0:T(8,128)(2,1)}, u32[]{:S(2)}, u32[]{:S(2)}) %collective-permute-start.5) | collective-permute-done | bytes 1572896 | tf_op jit(solution)/shard_map/ppermute | solution.py:32
  595.5 2.7 bitcast_dynamic-update-slice_fusion.1
  598.1 28.5 %collective-permute-done.6 = bf16[4,256,768]{2,1,0:T(8,128)(2,1)S(1)} collective-permute-done((bf16[4,256,768]{2,1,0:T(8,128)(2,1)}, bf16[4,256,768]{2,1,0:T(8,128)(2,1)S(1)}, u32[]{:S(2)}, u32[]{:S(2)}) %collective-permute-start.6) | collective-permute-done | bytes 1572896 | tf_op jit(solution)/shard_map/ppermute | solution.py:32
  626.7 1.2 bitcast_dynamic-update-slice_fusion
  627.9 11.2 %gather_fusion = bf16[8,4,256,768]{3,2,1,0:T(8,128)(2,1)} fusion(bf16[8,4,256,768]{3,2,1,0:T(8,128)(2,1)} %bitcast_dynamic-update-slice_fusion, s32[1024]{0:T(1024)S(1)} %pad_clamp_fusion), kind=kCustom, calls=%fused_computation | custom fusion | bytes 25165856 | tf_op jit(solution)/shard_map/gather | solution.py:37
  639.1 10.8 %copy.15 = bf16[4,8,256,768]{3,2,1,0:T(8,128)(2,1)} copy(bf16[4,8,256,768]{3,2,0,1:T(8,128)(2,1)} %bitcast.44) | data formatting | bytes 25165824 | tf_op jit(solution)/shard_map/transpose | solution.py:18
  649.9 16.6 %copy.17 = bf16[4,768,2048]{2,1,0:T(8,128)(2,1)} copy(bf16[4,768,2048]{1,2,0:T(8,128)(2,1)} %bitcast.42) | data formatting | bytes 25165824
  666.6 16.9 %copy.16 = bf16[8,4,256,768]{2,0,3,1:T(8,128)(2,1)} copy(bf16[8,4,256,768]{3,2,1,0:T(8,128)(2,1)} %bitcast.19) | data formatting | bytes 25165824 | tf_op jit(solution)/shard_map/all_to_all | solution.py:42
  683.4 19.5 %all_to_all.16 = bf16[4,2048,768]{1,2,0:T(8,128)(2,1)} reshape(bf16[4,8,256,768]{2,1,3,0:T(8,128)(2,1)} %bitcast.43) | data formatting | bytes 25165824 | tf_op jit(solution)/shard_map/all_to_all | solution.py:42
  (9 shorter events, 0.0 us)
Async XLA Ops:
  14.0 652.6 %all-to-all-start = ((bf16[32,256,768]{2,1,0:T(8,128)(2,1)}), bf16[32,256,768]{2,1,0:T(8,128)(2,1)}, u32[]{:S(2)}, u32[]{:S(2)}) async-start(bf16[32,256,768]{2,1,0:T(8,128)(2,1)} %convert_element_type.10), calls=%async_computation | async-start | bytes 25165824 | tf_op jit(solution)/shard_map/all_to_all | solution.py:42
  34.4 18.8 %copy-start = (f32[256,32]{0,1:T(8,128)S(1)}, f32[256,32]{0,1:T(8,128)}, u32[]{:S(2)}) copy-start(f32[256,32]{0,1:T(8,128)} %param.6) | copy-start | bytes 98308
  34.4 18.8 %copy-start.1 = (f32[256]{0:T(256)S(1)}, f32[256]{0:T(256)}, u32[]{:S(2)}) copy-start(f32[256]{0:T(256)} %param.7) | copy-start | bytes 3076
  43.5 514.4 %collective-permute-start = (bf16[4,256,768]{2,1,0:T(8,128)(2,1)S(1)}, bf16[4,256,768]{2,1,0:T(8,128)(2,1)}, u32[]{:S(2)}, u32[]{:S(2)}) collective-permute-start(bf16[4,256,768]{2,1,0:T(8,128)(2,1)S(1)} %get-tuple-element.15), channel_id=1, source_target_pairs={{0,1},{1,2},{2,3},{3,4},{4,5},{5,6},{6,7},{7,0},{8,9},{9,10},{10,1... | collective-permute-start | bytes 4718600 | tf_op jit(solution)/shard_map/ppermute | solution.py:32
  45.6 513.9 %collective-permute-start.1 = (bf16[4,256,768]{2,1,0:T(8,128)(2,1)}, bf16[4,256,768]{2,1,0:T(8,128)(2,1)}, u32[]{:S(2)}, u32[]{:S(2)}) collective-permute-start(bf16[4,256,768]{2,1,0:T(8,128)(2,1)} %get-tuple-element.14), channel_id=1, source_target_pairs={{0,2},{1,3},{2,4},{3,5},{4,6},{5,7},{6,0},{7,1},{8,10},{9,11},{10,... | collective-permute-start | bytes 4718600 | tf_op jit(solution)/shard_map/ppermute | solution.py:32
  47.0 517.7 %collective-permute-start.2 = (bf16[4,256,768]{2,1,0:T(8,128)(2,1)}, bf16[4,256,768]{2,1,0:T(8,128)(2,1)}, u32[]{:S(2)}, u32[]{:S(2)}) collective-permute-start(bf16[4,256,768]{2,1,0:T(8,128)(2,1)} %get-tuple-element.13), channel_id=1, source_target_pairs={{0,3},{1,4},{2,5},{3,6},{4,7},{5,0},{6,1},{7,2},{8,11},{9,12},{10,... | collective-permute-start | bytes 4718600 | tf_op jit(solution)/shard_map/ppermute | solution.py:32
  49.4 518.0 %collective-permute-start.3 = (bf16[4,256,768]{2,1,0:T(8,128)(2,1)}, bf16[4,256,768]{2,1,0:T(8,128)(2,1)}, u32[]{:S(2)}, u32[]{:S(2)}) collective-permute-start(bf16[4,256,768]{2,1,0:T(8,128)(2,1)} %get-tuple-element.12), channel_id=1, source_target_pairs={{0,4},{1,5},{2,6},{3,7},{4,0},{5,1},{6,2},{7,3},{8,12},{9,13},{10,... | collective-permute-start | bytes 4718600 | tf_op jit(solution)/shard_map/ppermute | solution.py:32
  50.9 519.2 %collective-permute-start.4 = (bf16[4,256,768]{2,1,0:T(8,128)(2,1)}, bf16[4,256,768]{2,1,0:T(8,128)(2,1)S(1)}, u32[]{:S(2)}, u32[]{:S(2)}) collective-permute-start(bf16[4,256,768]{2,1,0:T(8,128)(2,1)} %get-tuple-element.11), channel_id=1, source_target_pairs={{0,5},{1,6},{2,7},{3,0},{4,1},{5,2},{6,3},{7,4},{8,13},{9,14},{10,... | collective-permute-start | bytes 4718600 | tf_op jit(solution)/shard_map/ppermute | solution.py:32
  557.9 37.6 %collective-permute-start.5 = (bf16[4,256,768]{2,1,0:T(8,128)(2,1)}, bf16[4,256,768]{2,1,0:T(8,128)(2,1)}, u32[]{:S(2)}, u32[]{:S(2)}) collective-permute-start(bf16[4,256,768]{2,1,0:T(8,128)(2,1)} %get-tuple-element.10), channel_id=1, source_target_pairs={{0,6},{1,7},{2,0},{3,1},{4,2},{5,3},{6,4},{7,5},{8,14},{9,15},{10,... | collective-permute-start | bytes 4718600 | tf_op jit(solution)/shard_map/ppermute | solution.py:32
  559.5 67.2 %collective-permute-start.6 = (bf16[4,256,768]{2,1,0:T(8,128)(2,1)}, bf16[4,256,768]{2,1,0:T(8,128)(2,1)S(1)}, u32[]{:S(2)}, u32[]{:S(2)}) collective-permute-start(bf16[4,256,768]{2,1,0:T(8,128)(2,1)} %get-tuple-element.9), channel_id=1, source_target_pairs={{0,7},{1,0},{2,1},{3,2},{4,3},{5,4},{6,5},{7,6},{8,15},{9,8},{10,9... | collective-permute-start | bytes 4718600 | tf_op jit(solution)/shard_map/ppermute | solution.py:32
